TPU v7x, 32 devices: a whole 2x2x4 slice. The times are simulated.
32 devices in a mesh: gx: 4 (over y, core), gy: 2 (over x), gz: 4 (over z).
Axes of the slice: x: 2, y: 2, z: 4, core: 2. Of those that a mesh axis runs over, the one named last changes fastest.
Arguments:
- positions: float32 [4, 2, 8, 3, 128], P('gx', 'gy', 'gz'), may hold values from 0 to 256, as said below
- gaussian: float32 [4, 2, 8, 3, 128], P('gx', 'gy', 'gz'), may hold values from -120 to 120
- counts: int32 [4, 2, 8], P('gx', 'gy', 'gz'), may hold values from 32 to 128, as said below
Outputs:
- brownian: float32 [4, 2, 8, 3, 128], P('gx', 'gy', 'gz')
Inputs may be any that keep to these rules, and one draw needn't show every extreme that they name: `positions`: slot k of a cell lies within a quarter of 4 of its own lattice point in each component; the lattice points of all slots of all cells have spacing 4 and the cell of index (a, b, e) spans 4 points along the first two dimensions and 8 along the third from index 0 upward. Each cell's live particles are its first counts slots; every cell of the wall layer (third cell index 0) is full.
All inputs are finite; a program needn't handle non-finite values.
Results may differ from a plain program's by a relative error of at most 0.0003.
Values sent between devices are 32-bit elements; how exact they have to be, the bound alone decides.
A program may use at most 64 MiB of HBM per device.

v0:
```python
import jax
import jax.numpy as jnp
from jax import lax
from jax.sharding import PartitionSpec as P

wall_gap = 1.0
cell_offsets = ((0, 0, 0), (1, 0, 0), (-1, 0, 0), (0, 1, 0), (0, -1, 0), (0, 0, 1), (0, 0, -1))


def padded_2(array, sides, width):
    for axis, dim in sides:
        size, length = (lax.axis_size(axis), array.shape[dim])
        up = [(i, (i + 1) % size) for i in range(size - 1)]
        down = [(j, i) for i, j in up]
        last = lax.slice_in_dim(array, length - width, length, axis=dim)
        leading = lax.slice_in_dim(array, 0, width, axis=dim)
        before = lax.ppermute(last, axis, up)
        after = lax.ppermute(leading, axis, down)
        array = jnp.concatenate([before, array, after], axis=dim)
    return array


def pair_terms(target, source, values, self_pair):
    offset_vec = target[:, :, :, None] - source[:, :, None, :]
    distance_sq = jnp.sum(offset_vec * offset_vec, axis=1)
    width = target.shape[-1]
    diagonal = jnp.eye(width, dtype=bool)[None]
    if self_pair:
        distance_sq = jnp.where(diagonal, 1.0, distance_sq)
    inverse = lax.rsqrt(distance_sq)
    inv_cube = inverse * inverse * inverse
    isotropic = 0.75 * inverse + 0.5 * inv_cube
    dyadic = (0.75 * inverse - 1.5 * inv_cube) * inverse * inverse
    if self_pair:
        isotropic = jnp.where(diagonal, 0.0, isotropic)
        dyadic = jnp.where(diagonal, 0.0, dyadic)
    projected = jnp.sum(offset_vec * values[:, :, None, :], axis=1)
    direct = jnp.einsum("bij,bcj->bci", isotropic, values, precision=lax.Precision.HIGHEST)
    along_pair = jnp.sum(offset_vec * (dyadic * projected)[:, None], axis=3)
    return direct + along_pair


def wall_self(target, values):
    inv_height = 1.0 / (target[:, 2] + wall_gap)
    squared = inv_height * inv_height
    cubed = squared * inv_height
    fourth = squared * squared
    fifth = fourth * inv_height
    eleventh = fifth * fifth * inv_height
    twelfth = eleventh * inv_height
    parallel = 1.0 - 0.5625 * inv_height + 0.125 * cubed - 0.17578125 * fourth - 0.0625 * fifth
    perpend = (
        1.0
        - 1.125 * inv_height
        + 0.5 * cubed
        - 0.57 * fourth
        + 0.2 * fifth
        + 0.035 * eleventh
        - 0.04 * twelfth
    )
    mobility = jnp.stack([parallel, parallel, perpend], axis=1)
    return mobility * values


def cell_block(operands):
    target, sources, vectors, occupied = operands
    summed = wall_self(target, vectors[0])
    for neighbour in range(7):
        summed = summed + pair_terms(target, sources[neighbour], vectors[neighbour], neighbour == 0)
    return summed * occupied[:, None, :]


def stacked(padded, size_x, size_y, size_z):
    pieces = []
    for shift_x, shift_y, shift_z in cell_offsets:
        piece = padded[
            1 + shift_x : 1 + shift_x + size_x,
            1 + shift_y : 1 + shift_y + size_y,
            1 + shift_z : 1 + shift_z + size_z,
        ]
        pieces.append(piece.reshape((size_x * size_y, size_z) + piece.shape[3:]))
    return jnp.stack(pieces, axis=1)


def apply_mobility(padded_pos, padded_vec, occupied):
    size_x, size_y, size_z = (occupied.shape[0], occupied.shape[1], occupied.shape[2])
    width = occupied.shape[3]
    target = padded_pos[1:-1, 1:-1, 1:-1].reshape((size_x * size_y, size_z, 3, width))
    sources = stacked(padded_pos, size_x, size_y, size_z)
    vectors = stacked(padded_vec, size_x, size_y, size_z)
    live = occupied.reshape((size_x * size_y, size_z, width))
    result = lax.map(cell_block, (target, sources, vectors, live))
    return result.reshape((size_x, size_y, size_z, 3, width))


def vector_halo(vector):
    return padded_2(vector, (("gx", 0), ("gy", 1), ("gz", 2)), 1)


def shards(positions, gaussian, counts):
    width = positions.shape[-1]
    slot_index = jnp.arange(width, dtype=jnp.int32)
    occupied = (slot_index[None, None, None, :] < counts[:, :, :, None]).astype(jnp.float32)
    masked = gaussian * occupied[:, :, :, None, :]
    padded_pos = padded_2(positions, (("gx", 0), ("gy", 1), ("gz", 2)), 1)

    def mobility(vector):
        return apply_mobility(padded_pos, vector_halo(vector), occupied)

    mapped = mobility(masked)
    mapped_twice = mobility(mapped)
    noise_sq, cross_one, image_sq, cross_two = lax.psum(
        (
            jnp.sum(masked * masked),
            jnp.sum(masked * mapped),
            jnp.sum(mapped * mapped),
            jnp.sum(mapped * mapped_twice),
        ),
        ("gx", "gy", "gz"),
    )
    alpha_one = cross_one / noise_sq
    beta_sq = image_sq / noise_sq - alpha_one * alpha_one
    alpha_two = (cross_two - 2.0 * alpha_one * image_sq + alpha_one * alpha_one * cross_one) / (
        noise_sq * beta_sq
    )
    root_det = jnp.sqrt(alpha_one * alpha_two - beta_sq)
    trace_root = jnp.sqrt(alpha_one + alpha_two + 2.0 * root_det)
    return (alpha_one + root_det) / trace_root * masked + (mapped - alpha_one * masked) / trace_root


def solution(mesh):
    in_specs = (
        P("gx", "gy", "gz", None, None),
        P("gx", "gy", "gz", None, None),
        P("gx", "gy", "gz"),
    )
    out_specs = P("gx", "gy", "gz", None, None)
    return jax.shard_map(shards, mesh=mesh, in_specs=in_specs, out_specs=out_specs, check_vma=False)
```

profile of v0, /device:TPU:0, one launch (start us, length us, event | category | flops | bytes accessed | tf_op | source)
XLA Modules:
  0.0 118.0 jit_solution(7080927123905163732)
XLA Ops:
  0.0 0.7 copy-done.2
  0.7 1.3 %collective-permute-start = (f32[1,1,2,3,128]{4,2,3,1,0:T(2,128)S(1)}, f32[1,1,2,3,128]{4,2,3,1,0:T(2,128)S(1)}, u32[]{:S(2)}, u32[]{:S(2)}) collective-permute-start(f32[1,1,2,3,128]{4,2,3,1,0:T(2,128)S(1)} %broadcast_multiply_fusion), channel_id=1, source_target_pairs={{8,0},{16,8},{24,16},{9,1},{17,9},{25,17},{10,2},{18,10},{26,18},{... | collective-permute-start | bytes 9224 | tf_op jit(solution)/shard_map/ppermute | solution.py:18
  2.0 3.0 %collective-permute-start.2 = (f32[1,1,2,3,128]{4,2,3,1,0:T(2,128)S(1)}, f32[1,1,2,3,128]{4,2,3,1,0:T(2,128)S(1)}, u32[]{:S(2)}, u32[]{:S(2)}) collective-permute-start(f32[1,1,2,3,128]{4,2,3,1,0:T(2,128)S(1)} %broadcast_multiply_fusion), channel_id=1, source_target_pairs={{0,8},{8,16},{16,24},{1,9},{9,17},{17,25},{2,10},{10,18},{18,26},{... | collective-permute-start | bytes 9224 | tf_op jit(solution)/shard_map/ppermute | solution.py:17
  5.1 4.5 %collective-permute-start.3 = (f32[1,1,2,3,128]{4,2,3,1,0:T(2,128)S(1)}, f32[1,1,2,3,128]{4,2,3,1,0:T(2,128)S(1)}, u32[]{:S(2)}, u32[]{:S(2)}) collective-permute-start(f32[1,1,2,3,128]{4,2,3,1,0:T(2,128)S(1)} %copy-done.1), channel_id=1, source_target_pairs={{0,8},{8,16},{16,24},{1,9},{9,17},{17,25},{2,10},{10,18},{18,26},{... | collective-permute-start | bytes 9224 | tf_op jit(solution)/shard_map/ppermute | solution.py:17
  9.6 1.3 %collective-permute-start.1 = (f32[1,1,2,3,128]{4,2,3,1,0:T(2,128)S(1)}, f32[1,1,2,3,128]{4,2,3,1,0:T(2,128)S(1)}, u32[]{:S(2)}, u32[]{:S(2)}) collective-permute-start(f32[1,1,2,3,128]{4,2,3,1,0:T(2,128)S(1)} %copy-done.1), channel_id=1, source_target_pairs={{8,0},{16,8},{24,16},{9,1},{17,9},{25,17},{10,2},{18,10},{26,18},{... | collective-permute-start | bytes 9224 | tf_op jit(solution)/shard_map/ppermute | solution.py:18
  11.0 1.3 %collective-permute-start.4 = (f32[3,1,2,3,128]{4,2,3,1,0:T(2,128)S(1)}, f32[3,1,2,3,128]{4,2,3,1,0:T(2,128)S(1)}, u32[]{:S(2)}, u32[]{:S(2)}) collective-permute-start(f32[3,1,2,3,128]{4,2,3,1,0:T(2,128)S(1)} %pad_maximum_fusion.3), channel_id=1, source_target_pairs={{4,0},{5,1},{6,2},{7,3},{12,8},{13,9},{14,10},{15,11},{20,16},{21,... | collective-permute-start | bytes 27656 | tf_op jit(solution)/shard_map/ppermute | solution.py:18
  12.3 4.5 %collective-permute-start.6 = (f32[3,1,2,3,128]{4,2,3,1,0:T(2,128)S(1)}, f32[3,1,2,3,128]{4,2,3,1,0:T(2,128)S(1)}, u32[]{:S(2)}, u32[]{:S(2)}) collective-permute-start(f32[3,1,2,3,128]{4,2,3,1,0:T(2,128)S(1)} %pad_maximum_fusion.3), channel_id=1, source_target_pairs={{0,4},{1,5},{2,6},{3,7},{8,12},{9,13},{10,14},{11,15},{16,20},{17,... | collective-permute-start | bytes 27656 | tf_op jit(solution)/shard_map/ppermute | solution.py:17
  16.9 1.3 %collective-permute-start.5 = (f32[3,1,2,3,128]{4,2,3,1,0:T(2,128)S(1)}, f32[3,1,2,3,128]{4,2,3,1,0:T(2,128)S(1)}, u32[]{:S(2)}, u32[]{:S(2)}) collective-permute-start(f32[3,1,2,3,128]{4,2,3,1,0:T(2,128)S(1)} %constant_dynamic-update-slice_fusion), channel_id=1, source_target_pairs={{4,0},{5,1},{6,2},{7,3},{12,8},{13,9},{14,10},{15,11},{20,16},{21,... | collective-permute-start | bytes 27656 | tf_op jit(solution)/shard_map/ppermute | solution.py:18
  18.2 4.5 %collective-permute-start.7 = (f32[3,1,2,3,128]{4,2,3,1,0:T(2,128)S(1)}, f32[3,1,2,3,128]{4,2,3,1,0:T(2,128)S(1)}, u32[]{:S(2)}, u32[]{:S(2)}) collective-permute-start(f32[3,1,2,3,128]{4,2,3,1,0:T(2,128)S(1)} %constant_dynamic-update-slice_fusion), channel_id=1, source_target_pairs={{0,4},{1,5},{2,6},{3,7},{8,12},{9,13},{10,14},{11,15},{16,20},{17,... | collective-permute-start | bytes 27656 | tf_op jit(solution)/shard_map/ppermute | solution.py:17
  22.9 3.5 %collective-permute-start.10 = (f32[3,3,1,3,128]{4,2,3,1,0:T(1,128)S(1)}, f32[3,3,1,3,128]{4,2,3,1,0:T(1,128)S(1)}, u32[]{:S(2)}, u32[]{:S(2)}) collective-permute-start(f32[3,3,1,3,128]{4,2,3,1,0:T(1,128)S(1)} %get-tuple-element.107), channel_id=1, source_target_pairs={{0,1},{1,2},{2,3},{4,5},{5,6},{6,7},{8,9},{9,10},{10,11},{12,13},{... | collective-permute-start | bytes 41480 | tf_op jit(solution)/shard_map/ppermute | solution.py:17
  26.4 1.3 %collective-permute-start.8 = (f32[3,3,1,3,128]{4,2,3,1,0:T(1,128)S(1)}, f32[3,3,1,3,128]{4,2,3,1,0:T(1,128)S(1)}, u32[]{:S(2)}, u32[]{:S(2)}) collective-permute-start(f32[3,3,1,3,128]{4,2,3,1,0:T(1,128)S(1)} %get-tuple-element.108), channel_id=1, source_target_pairs={{1,0},{2,1},{3,2},{5,4},{6,5},{7,6},{9,8},{10,9},{11,10},{13,12},{... | collective-permute-start | bytes 41480 | tf_op jit(solution)/shard_map/ppermute | solution.py:18
  27.8 4.5 %collective-permute-start.11 = (f32[3,3,1,3,128]{4,2,3,1,0:T(1,128)S(1)}, f32[3,3,1,3,128]{4,2,3,1,0:T(1,128)S(1)}, u32[]{:S(2)}, u32[]{:S(2)}) collective-permute-start(f32[3,3,1,3,128]{4,2,3,1,0:T(1,128)S(1)} %get-tuple-element.103), channel_id=1, source_target_pairs={{0,1},{1,2},{2,3},{4,5},{5,6},{6,7},{8,9},{9,10},{10,11},{12,13},{... | collective-permute-start | bytes 41480 | tf_op jit(solution)/shard_map/ppermute | solution.py:17
  32.3 1.3 %collective-permute-start.9 = (f32[3,3,1,3,128]{4,2,3,1,0:T(1,128)S(1)}, f32[3,3,1,3,128]{4,2,3,1,0:T(1,128)S(1)}, u32[]{:S(2)}, u32[]{:S(2)}) collective-permute-start(f32[3,3,1,3,128]{4,2,3,1,0:T(1,128)S(1)} %get-tuple-element.104), channel_id=1, source_target_pairs={{1,0},{2,1},{3,2},{5,4},{6,5},{7,6},{9,8},{10,9},{11,10},{13,12},{... | collective-permute-start | bytes 41480 | tf_op jit(solution)/shard_map/ppermute | solution.py:18
  33.7 4.2 %collective-permute-done.9 = f32[3,3,1,3,128]{4,2,3,1,0:T(1,128)S(1)} collective-permute-done((f32[3,3,1,3,128]{4,2,3,1,0:T(1,128)S(1)}, f32[3,3,1,3,128]{4,2,3,1,0:T(1,128)S(1)}, u32[]{:S(2)}, u32[]{:S(2)}) %collective-permute-start.9) | collective-permute-done | bytes 13856 | tf_op jit(solution)/shard_map/ppermute | solution.py:18
  38.0 0.5 fusion.5
  38.5 0.3 fusion.41
  38.9 0.3 fusion.43
  39.3 0.3 fusion.45
  39.7 0.3 fusion.47
  40.1 0.3 fusion.37
  40.5 0.3 fusion.61
  40.9 0.5 fusion.10
  41.4 0.3 fusion.39
  41.8 0.8 fusion.12
  42.6 0.7 multiply_reduce_fusion.1
  43.3 1.3 %collective-permute-start.13 = (f32[1,1,2,3,128]{4,2,3,1,0:T(2,128)S(1)}, f32[1,1,2,3,128]{4,2,3,1,0:T(2,128)S(1)}, u32[]{:S(2)}, u32[]{:S(2)}) collective-permute-start(f32[1,1,2,3,128]{4,2,3,1,0:T(2,128)S(1)} %bitcast.39), channel_id=1, source_target_pairs={{0,8},{8,16},{16,24},{1,9},{9,17},{17,25},{2,10},{10,18},{18,26},{... | collective-permute-start | bytes 9224 | tf_op jit(solution)/shard_map/ppermute | solution.py:17
  44.6 1.3 %collective-permute-start.12 = (f32[1,1,2,3,128]{4,2,3,1,0:T(2,128)S(1)}, f32[1,1,2,3,128]{4,2,3,1,0:T(2,128)S(1)}, u32[]{:S(2)}, u32[]{:S(2)}) collective-permute-start(f32[1,1,2,3,128]{4,2,3,1,0:T(2,128)S(1)} %bitcast.40), channel_id=1, source_target_pairs={{8,0},{16,8},{24,16},{9,1},{17,9},{25,17},{10,2},{18,10},{26,18},{... | collective-permute-start | bytes 9224 | tf_op jit(solution)/shard_map/ppermute | solution.py:18
  45.9 0.3 fusion.60
  46.2 4.4 %collective-permute-done.12 = f32[1,1,2,3,128]{4,2,3,1,0:T(2,128)S(1)} collective-permute-done((f32[1,1,2,3,128]{4,2,3,1,0:T(2,128)S(1)}, f32[1,1,2,3,128]{4,2,3,1,0:T(2,128)S(1)}, u32[]{:S(2)}, u32[]{:S(2)}) %collective-permute-start.12) | collective-permute-done | bytes 3104 | tf_op jit(solution)/shard_map/ppermute | solution.py:18
  50.7 1.3 %collective-permute-start.14 = (f32[3,1,2,3,128]{4,2,3,1,0:T(2,128)S(1)}, f32[3,1,2,3,128]{4,2,3,1,0:T(2,128)S(1)}, u32[]{:S(2)}, u32[]{:S(2)}) collective-permute-start(f32[3,1,2,3,128]{4,2,3,1,0:T(2,128)S(1)} %pad_maximum_fusion.4), channel_id=1, source_target_pairs={{4,0},{5,1},{6,2},{7,3},{12,8},{13,9},{14,10},{15,11},{20,16},{21,... | collective-permute-start | bytes 27656 | tf_op jit(solution)/shard_map/ppermute | solution.py:18
  51.9 4.5 %collective-permute-start.15 = (f32[3,1,2,3,128]{4,2,3,1,0:T(2,128)S(1)}, f32[3,1,2,3,128]{4,2,3,1,0:T(2,128)S(1)}, u32[]{:S(2)}, u32[]{:S(2)}) collective-permute-start(f32[3,1,2,3,128]{4,2,3,1,0:T(2,128)S(1)} %pad_maximum_fusion.4), channel_id=1, source_target_pairs={{0,4},{1,5},{2,6},{3,7},{8,12},{9,13},{10,14},{11,15},{16,20},{17,... | collective-permute-start | bytes 27656 | tf_op jit(solution)/shard_map/ppermute | solution.py:17
  56.5 0.3 fusion.38
  56.8 1.0 collective-permute-done.15
  57.9 1.3 %collective-permute-start.16 = (f32[3,3,1,3,128]{4,2,3,1,0:T(1,128)S(1)}, f32[3,3,1,3,128]{4,2,3,1,0:T(1,128)S(1)}, u32[]{:S(2)}, u32[]{:S(2)}) collective-permute-start(f32[3,3,1,3,128]{4,2,3,1,0:T(1,128)S(1)} %get-tuple-element.99), channel_id=1, source_target_pairs={{1,0},{2,1},{3,2},{5,4},{6,5},{7,6},{9,8},{10,9},{11,10},{13,12},{... | collective-permute-start | bytes 41480 | tf_op jit(solution)/shard_map/ppermute | solution.py:18
  59.2 4.5 %collective-permute-start.17 = (f32[3,3,1,3,128]{4,2,3,1,0:T(1,128)S(1)}, f32[3,3,1,3,128]{4,2,3,1,0:T(1,128)S(1)}, u32[]{:S(2)}, u32[]{:S(2)}) collective-permute-start(f32[3,3,1,3,128]{4,2,3,1,0:T(1,128)S(1)} %get-tuple-element.100), channel_id=1, source_target_pairs={{0,1},{1,2},{2,3},{4,5},{5,6},{6,7},{8,9},{9,10},{10,11},{12,13},{... | collective-permute-start | bytes 41480 | tf_op jit(solution)/shard_map/ppermute | solution.py:17
  63.8 0.3 fusion.36
  64.1 1.1 collective-permute-done.17
  65.2 0.3 fusion.40
  65.5 0.3 fusion.42
  65.8 0.3 fusion.44
  66.2 0.3 fusion.46
  66.5 0.4 fusion.3
  67.1 0.1 fusion.54
  67.2 0.1 fusion.58
  67.3 1.0 fusion.4
  68.3 0.7 multiply_reduce_fusion
  69.0 43.1 %all-reduce = (f32[]{:T(128)}, f32[]{:T(128)}, f32[]{:T(128)}, f32[]{:T(128)}) all-reduce(f32[]{:T(128)} %get-tuple-element.89, f32[]{:T(128)} %get-tuple-element.88, f32[]{:T(128)} %get-tuple-element.87, f32[]{:T(128)} %get-tuple-element.86), channel_id=1, replica_groups=mesh['gx'=4,'gy'=2,'gz'=4] {'gx','gy','gz'}, use_global_device_ids=true, to_apply=%region_22.23 | all-reduce | flops 4 | bytes 32 | tf_op jit(solution)/shard_map/psum | solution.py:112
  117.4 0.6 divide_add_fusion
  (69 shorter events, 1.1 us)
Async XLA Ops:
  0.0 0.7 copy-start.2
  0.0 0.7 copy-start
  0.7 4.3 %copy-start.1 = (f32[1,1,2,3,128]{4,2,3,1,0:T(2,128)S(1)}, f32[1,1,2,3,128]{4,2,3,1,0:T(2,128)}, u32[]{:S(2)}) copy-start(f32[1,1,2,3,128]{4,2,3,1,0:T(2,128)} %param.3) | copy-start | bytes 9220
  0.7 10.3 %collective-permute-start = (f32[1,1,2,3,128]{4,2,3,1,0:T(2,128)S(1)}, f32[1,1,2,3,128]{4,2,3,1,0:T(2,128)S(1)}, u32[]{:S(2)}, u32[]{:S(2)}) collective-permute-start(f32[1,1,2,3,128]{4,2,3,1,0:T(2,128)S(1)} %broadcast_multiply_fusion), channel_id=1, source_target_pairs={{8,0},{16,8},{24,16},{9,1},{17,9},{25,17},{10,2},{18,10},{26,18},{... | collective-permute-start | bytes 9224 | tf_op jit(solution)/shard_map/ppermute | solution.py:18
  2.0 9.0 %collective-permute-start.2 = (f32[1,1,2,3,128]{4,2,3,1,0:T(2,128)S(1)}, f32[1,1,2,3,128]{4,2,3,1,0:T(2,128)S(1)}, u32[]{:S(2)}, u32[]{:S(2)}) collective-permute-start(f32[1,1,2,3,128]{4,2,3,1,0:T(2,128)S(1)} %broadcast_multiply_fusion), channel_id=1, source_target_pairs={{0,8},{8,16},{16,24},{1,9},{9,17},{17,25},{2,10},{10,18},{18,26},{... | collective-permute-start | bytes 9224 | tf_op jit(solution)/shard_map/ppermute | solution.py:17
  5.1 11.8 %collective-permute-start.3 = (f32[1,1,2,3,128]{4,2,3,1,0:T(2,128)S(1)}, f32[1,1,2,3,128]{4,2,3,1,0:T(2,128)S(1)}, u32[]{:S(2)}, u32[]{:S(2)}) collective-permute-start(f32[1,1,2,3,128]{4,2,3,1,0:T(2,128)S(1)} %copy-done.1), channel_id=1, source_target_pairs={{0,8},{8,16},{16,24},{1,9},{9,17},{17,25},{2,10},{10,18},{18,26},{... | collective-permute-start | bytes 9224 | tf_op jit(solution)/shard_map/ppermute | solution.py:17
  9.6 7.3 %collective-permute-start.1 = (f32[1,1,2,3,128]{4,2,3,1,0:T(2,128)S(1)}, f32[1,1,2,3,128]{4,2,3,1,0:T(2,128)S(1)}, u32[]{:S(2)}, u32[]{:S(2)}) collective-permute-start(f32[1,1,2,3,128]{4,2,3,1,0:T(2,128)S(1)} %copy-done.1), channel_id=1, source_target_pairs={{8,0},{16,8},{24,16},{9,1},{17,9},{25,17},{10,2},{18,10},{26,18},{... | collective-permute-start | bytes 9224 | tf_op jit(solution)/shard_map/ppermute | solution.py:18
  11.0 11.8 %collective-permute-start.4 = (f32[3,1,2,3,128]{4,2,3,1,0:T(2,128)S(1)}, f32[3,1,2,3,128]{4,2,3,1,0:T(2,128)S(1)}, u32[]{:S(2)}, u32[]{:S(2)}) collective-permute-start(f32[3,1,2,3,128]{4,2,3,1,0:T(2,128)S(1)} %pad_maximum_fusion.3), channel_id=1, source_target_pairs={{4,0},{5,1},{6,2},{7,3},{12,8},{13,9},{14,10},{15,11},{20,16},{21,... | collective-permute-start | bytes 27656 | tf_op jit(solution)/shard_map/ppermute | solution.py:18
  12.3 10.5 %collective-permute-start.6 = (f32[3,1,2,3,128]{4,2,3,1,0:T(2,128)S(1)}, f32[3,1,2,3,128]{4,2,3,1,0:T(2,128)S(1)}, u32[]{:S(2)}, u32[]{:S(2)}) collective-permute-start(f32[3,1,2,3,128]{4,2,3,1,0:T(2,128)S(1)} %pad_maximum_fusion.3), channel_id=1, source_target_pairs={{0,4},{1,5},{2,6},{3,7},{8,12},{9,13},{10,14},{11,15},{16,20},{17,... | collective-permute-start | bytes 27656 | tf_op jit(solution)/shard_map/ppermute | solution.py:17
  16.9 10.8 %collective-permute-start.5 = (f32[3,1,2,3,128]{4,2,3,1,0:T(2,128)S(1)}, f32[3,1,2,3,128]{4,2,3,1,0:T(2,128)S(1)}, u32[]{:S(2)}, u32[]{:S(2)}) collective-permute-start(f32[3,1,2,3,128]{4,2,3,1,0:T(2,128)S(1)} %constant_dynamic-update-slice_fusion), channel_id=1, source_target_pairs={{4,0},{5,1},{6,2},{7,3},{12,8},{13,9},{14,10},{15,11},{20,16},{21,... | collective-permute-start | bytes 27656 | tf_op jit(solution)/shard_map/ppermute | solution.py:18
  18.2 9.5 %collective-permute-start.7 = (f32[3,1,2,3,128]{4,2,3,1,0:T(2,128)S(1)}, f32[3,1,2,3,128]{4,2,3,1,0:T(2,128)S(1)}, u32[]{:S(2)}, u32[]{:S(2)}) collective-permute-start(f32[3,1,2,3,128]{4,2,3,1,0:T(2,128)S(1)} %constant_dynamic-update-slice_fusion), channel_id=1, source_target_pairs={{0,4},{1,5},{2,6},{3,7},{8,12},{9,13},{10,14},{11,15},{16,20},{17,... | collective-permute-start | bytes 27656 | tf_op jit(solution)/shard_map/ppermute | solution.py:17
  22.9 10.7 %collective-permute-start.10 = (f32[3,3,1,3,128]{4,2,3,1,0:T(1,128)S(1)}, f32[3,3,1,3,128]{4,2,3,1,0:T(1,128)S(1)}, u32[]{:S(2)}, u32[]{:S(2)}) collective-permute-start(f32[3,3,1,3,128]{4,2,3,1,0:T(1,128)S(1)} %get-tuple-element.107), channel_id=1, source_target_pairs={{0,1},{1,2},{2,3},{4,5},{5,6},{6,7},{8,9},{9,10},{10,11},{12,13},{... | collective-permute-start | bytes 41480 | tf_op jit(solution)/shard_map/ppermute | solution.py:17
  26.4 7.2 %collective-permute-start.8 = (f32[3,3,1,3,128]{4,2,3,1,0:T(1,128)S(1)}, f32[3,3,1,3,128]{4,2,3,1,0:T(1,128)S(1)}, u32[]{:S(2)}, u32[]{:S(2)}) collective-permute-start(f32[3,3,1,3,128]{4,2,3,1,0:T(1,128)S(1)} %get-tuple-element.108), channel_id=1, source_target_pairs={{1,0},{2,1},{3,2},{5,4},{6,5},{7,6},{9,8},{10,9},{11,10},{13,12},{... | collective-permute-start | bytes 41480 | tf_op jit(solution)/shard_map/ppermute | solution.py:18
  27.8 6.0 %collective-permute-start.11 = (f32[3,3,1,3,128]{4,2,3,1,0:T(1,128)S(1)}, f32[3,3,1,3,128]{4,2,3,1,0:T(1,128)S(1)}, u32[]{:S(2)}, u32[]{:S(2)}) collective-permute-start(f32[3,3,1,3,128]{4,2,3,1,0:T(1,128)S(1)} %get-tuple-element.103), channel_id=1, source_target_pairs={{0,1},{1,2},{2,3},{4,5},{5,6},{6,7},{8,9},{9,10},{10,11},{12,13},{... | collective-permute-start | bytes 41480 | tf_op jit(solution)/shard_map/ppermute | solution.py:17
  32.3 5.6 %collective-permute-start.9 = (f32[3,3,1,3,128]{4,2,3,1,0:T(1,128)S(1)}, f32[3,3,1,3,128]{4,2,3,1,0:T(1,128)S(1)}, u32[]{:S(2)}, u32[]{:S(2)}) collective-permute-start(f32[3,3,1,3,128]{4,2,3,1,0:T(1,128)S(1)} %get-tuple-element.104), channel_id=1, source_target_pairs={{1,0},{2,1},{3,2},{5,4},{6,5},{7,6},{9,8},{10,9},{11,10},{13,12},{... | collective-permute-start | bytes 41480 | tf_op jit(solution)/shard_map/ppermute | solution.py:18
  43.3 2.9 %collective-permute-start.13 = (f32[1,1,2,3,128]{4,2,3,1,0:T(2,128)S(1)}, f32[1,1,2,3,128]{4,2,3,1,0:T(2,128)S(1)}, u32[]{:S(2)}, u32[]{:S(2)}) collective-permute-start(f32[1,1,2,3,128]{4,2,3,1,0:T(2,128)S(1)} %bitcast.39), channel_id=1, source_target_pairs={{0,8},{8,16},{16,24},{1,9},{9,17},{17,25},{2,10},{10,18},{18,26},{... | collective-permute-start | bytes 9224 | tf_op jit(solution)/shard_map/ppermute | solution.py:17
  44.6 6.0 %collective-permute-start.12 = (f32[1,1,2,3,128]{4,2,3,1,0:T(2,128)S(1)}, f32[1,1,2,3,128]{4,2,3,1,0:T(2,128)S(1)}, u32[]{:S(2)}, u32[]{:S(2)}) collective-permute-start(f32[1,1,2,3,128]{4,2,3,1,0:T(2,128)S(1)} %bitcast.40), channel_id=1, source_target_pairs={{8,0},{16,8},{24,16},{9,1},{17,9},{25,17},{10,2},{18,10},{26,18},{... | collective-permute-start | bytes 9224 | tf_op jit(solution)/shard_map/ppermute | solution.py:18
  50.7 6.2 %collective-permute-start.14 = (f32[3,1,2,3,128]{4,2,3,1,0:T(2,128)S(1)}, f32[3,1,2,3,128]{4,2,3,1,0:T(2,128)S(1)}, u32[]{:S(2)}, u32[]{:S(2)}) collective-permute-start(f32[3,1,2,3,128]{4,2,3,1,0:T(2,128)S(1)} %pad_maximum_fusion.4), channel_id=1, source_target_pairs={{4,0},{5,1},{6,2},{7,3},{12,8},{13,9},{14,10},{15,11},{20,16},{21,... | collective-permute-start | bytes 27656 | tf_op jit(solution)/shard_map/ppermute | solution.py:18
  51.9 5.9 %collective-permute-start.15 = (f32[3,1,2,3,128]{4,2,3,1,0:T(2,128)S(1)}, f32[3,1,2,3,128]{4,2,3,1,0:T(2,128)S(1)}, u32[]{:S(2)}, u32[]{:S(2)}) collective-permute-start(f32[3,1,2,3,128]{4,2,3,1,0:T(2,128)S(1)} %pad_maximum_fusion.4), channel_id=1, source_target_pairs={{0,4},{1,5},{2,6},{3,7},{8,12},{9,13},{10,14},{11,15},{16,20},{17,... | collective-permute-start | bytes 27656 | tf_op jit(solution)/shard_map/ppermute | solution.py:17
  57.9 6.2 %collective-permute-start.16 = (f32[3,3,1,3,128]{4,2,3,1,0:T(1,128)S(1)}, f32[3,3,1,3,128]{4,2,3,1,0:T(1,128)S(1)}, u32[]{:S(2)}, u32[]{:S(2)}) collective-permute-start(f32[3,3,1,3,128]{4,2,3,1,0:T(1,128)S(1)} %get-tuple-element.99), channel_id=1, source_target_pairs={{1,0},{2,1},{3,2},{5,4},{6,5},{7,6},{9,8},{10,9},{11,10},{13,12},{... | collective-permute-start | bytes 41480 | tf_op jit(solution)/shard_map/ppermute | solution.py:18
  59.2 6.0 %collective-permute-start.17 = (f32[3,3,1,3,128]{4,2,3,1,0:T(1,128)S(1)}, f32[3,3,1,3,128]{4,2,3,1,0:T(1,128)S(1)}, u32[]{:S(2)}, u32[]{:S(2)}) collective-permute-start(f32[3,3,1,3,128]{4,2,3,1,0:T(1,128)S(1)} %get-tuple-element.100), channel_id=1, source_target_pairs={{0,1},{1,2},{2,3},{4,5},{5,6},{6,7},{8,9},{9,10},{10,11},{12,13},{... | collective-permute-start | bytes 41480 | tf_op jit(solution)/shard_map/ppermute | solution.py:17
where the time goes:
time: 119 us; the launch traced here: 118 us
  starting transfers between devices  46.7 us (39%)
  blocking collectives  43.1 us (36%)
  waiting for transfers between devices  10.8 us (9%)
  other arithmetic  6.26 us (5%)
  between operations  5.87 us (5%)
  matrix products  4.54 us (4%)
    psum x1, blocking collectives, shards(): lax.psum((jnp.sum(masked * masked), jnp.sum(masked * mapped), jnp.sum(map...  43.1 us
    ppermute x9, starting transfers between devices, padded_2(): before = lax.ppermute(last, axis, up)  35 us
    ppermute x9, starting transfers between devices, padded_2(): after = lax.ppermute(leading, axis, down)  11.6 us
    ppermute x9, waiting for transfers between devices, padded_2(): after = lax.ppermute(leading, axis, down)  8.64 us
    dot_general x14, matrix products, pair_terms(): jnp.einsum('bij,bcj->bci', isotropic, values, precision=lax.Precision.HIG...  4.54 us
  transfers between devices with their start and end apart: 18, of which 4 were waited for; matrix products, arithmetic and copies ran while one was open for 1% of the time, Pallas kernels for 0%

commit v1 on v0

v1 whole, which is shorter than its diff:
```python
import functools
import itertools

import jax
import jax.numpy as jnp
from jax import lax
from jax.experimental import pallas as pl
from jax.experimental.pallas import tpu as pltpu
from jax.sharding import PartitionSpec as P

wall_gap = 1.0
lanes = 8
direct_limit = 64
far_away = -4096.0
names = ("gx", "gy", "gz")


def groups_of(sizes):
    total = sizes[0] * sizes[1] * sizes[2]
    return [(0, 1, 2)] if total <= direct_limit else [(0,), (1,), (2,)]


def stage_offsets(sizes, axes):
    ranges = [range(sizes[k]) if k in axes else range(1) for k in range(3)]
    return [offset for offset in itertools.product(*ranges) if any(offset)]


def shifted(here, sizes, offset):
    return tuple(
        lax.rem(here[k] + offset[k], sizes[k]) if offset[k] else here[k] for k in range(3)
    )


def wall_mobility(height):
    inv_height = 1.0 / (height + wall_gap)
    squared = inv_height * inv_height
    cubed = squared * inv_height
    fourth = squared * squared
    fifth = fourth * inv_height
    eleventh = fifth * fifth * inv_height
    twelfth = eleventh * inv_height
    parallel = 1.0 - 0.5625 * inv_height + 0.125 * cubed - 0.17578125 * fourth - 0.0625 * fifth
    perpend = (
        1.0
        - 1.125 * inv_height
        + 0.5 * cubed
        - 0.57 * fourth
        + 0.2 * fifth
        + 0.035 * eleventh
        - 0.04 * twelfth
    )
    return parallel, parallel, perpend


def kernel(
    sizes, local, width, counts_ref, pos_ref, gauss_ref, out_ref,
    packed, mapped, halo_x, halo_y, halo_z, next_x, next_y, next_z,
    column, image_column, acc, iso, dyad, sums,
    send_one, recv_one, send_two, recv_two, send_sum, recv_sum,
):
    here = tuple(lax.axis_index(name) for name in names)
    cells = list(itertools.product(*(range(size) for size in local)))
    halos, nexts = (halo_x, halo_y, halo_z), (next_x, next_y, next_z)
    stages = groups_of(sizes)
    offsets = [stage_offsets(sizes, axes) for axes in stages]
    faces = [(axis, side) for axis in range(3) if sizes[axis] > 1 for side in range(2)]
    groups = width // lanes

    def exists(axis, side):
        return here[axis] < sizes[axis] - 1 if side else here[axis] > 0

    def slab(axis, side):
        index = [slice(None)] * 3
        index[axis] = pl.ds(local[axis] - 1 if side else 0, 1)
        return tuple(index)

    def beside(axis, side):
        return {names[axis]: here[axis] + (1 if side else -1)}

    zero_tile = jnp.zeros((lanes, width), jnp.float32)
    tile_row = lax.broadcasted_iota(jnp.int32, (lanes, width), 0)
    outside = jnp.where(tile_row < 3, far_away, 0.0)
    for axis in range(3):
        face_cells = [c for c in cells if c[axis] == 0]
        for side in range(2):
            def clear(axis=axis, side=side, face_cells=face_cells):
                for cell in face_cells:
                    halos[axis][(side,) + cell] = outside
                    if side:
                        nexts[axis][cell] = zero_tile
            pl.when(jnp.logical_not(exists(axis, side)))(clear)

    barrier = pltpu.get_barrier_semaphore()
    peers = [offset for stage in offsets for offset in stage]
    for offset in peers:
        pl.semaphore_signal(
            barrier, inc=1, device_id=shifted(here, sizes, offset),
            device_id_type=pl.DeviceIdType.MESH,
        )

    lane = lax.broadcasted_iota(jnp.int32, (1, width), 1)
    occupied, walls = {}, {}
    for cell in cells:
        occupied[cell] = (lane < counts_ref[cell]).astype(jnp.float32)
        position = pos_ref[cell]
        packed[cell + (pl.ds(0, 3),)] = position
        packed[cell + (pl.ds(3, 3),)] = gauss_ref[cell] * occupied[cell]
        packed[cell + (pl.ds(6, 2),)] = jnp.zeros((2, width), jnp.float32)
        walls[cell] = wall_mobility(position[2:3])

    def row(ref, index, which):
        return ref[index + (pl.ds(which, 1),)]

    def spread(ref, cell, values):
        for which in range(3):
            full = jnp.broadcast_to(values[which], (width, width))
            ref[cell + (which,)] = full.T

    for cell in cells:
        spread(column, cell, [row(packed, cell, which) for which in range(3)])

    def source_of(cell, axis, side):
        there = list(cell)
        there[axis] += 1 if side else -1
        if 0 <= there[axis] < local[axis]:
            return packed, tuple(there), False
        there[axis] = 0
        return halos[axis], (side,) + tuple(there), True

    inner, outer, saved = {}, {}, []
    for cell in cells:
        inner[cell] = [(packed, cell, None)]
        outer[cell] = []
        saved.append((cell, None))
        for axis in range(3):
            for side in range(2):
                ref, index, remote = source_of(cell, axis, side)
                if remote and sizes[axis] == 1:
                    continue
                (outer if remote else inner)[cell].append((ref, index, (axis, side)))
                if side:
                    saved.append((cell, axis))
    slot_of = {key: slot for slot, key in enumerate(saved)}

    def diagonal(group):
        rows = group * lanes + lax.broadcasted_iota(jnp.int32, (lanes, width), 0)
        return rows == lax.broadcasted_iota(jnp.int32, (lanes, width), 1)

    def first_product(table, start):
        def body(group, carry):
            rows = pl.ds(pl.multiple_of(group * lanes, lanes), lanes)
            for cell in cells:
                target = [column[cell + (which, rows)] for which in range(3)]
                total = None if start else [acc[cell + (which, rows)] for which in range(3)]
                for ref, index, direction in table[cell]:
                    delta = [target[which] - row(ref, index, which) for which in range(3)]
                    value = [row(ref, index, 3 + which) for which in range(3)]
                    square = delta[0] * delta[0] + delta[1] * delta[1] + delta[2] * delta[2]
                    inverse = lax.rsqrt(square)
                    if direction is None:
                        inverse = jnp.where(diagonal(group), 0.0, inverse)
                    inv_sq = inverse * inverse
                    isotropic = inverse * (0.75 + 0.5 * inv_sq)
                    dyadic = (inverse * inv_sq) * (0.75 - 1.5 * inv_sq)
                    if direction is None or direction[1]:
                        slot = slot_of[(cell, None if direction is None else direction[0])]
                        iso[slot, rows] = isotropic
                        dyad[slot, rows] = dyadic
                    scaled = dyadic * (
                        delta[0] * value[0] + delta[1] * value[1] + delta[2] * value[2]
                    )
                    part = [isotropic * value[which] + delta[which] * scaled for which in range(3)]
                    total = part if total is None else [a + b for a, b in zip(total, part)]
                for which in range(3):
                    acc[cell + (which, rows)] = total[which]
            return carry

        lax.fori_loop(0, groups, body, 0)

    first_product(inner, True)

    pl.semaphore_wait(barrier, len(peers))

    def halo_copy(axis, side, receiver):
        held = side if receiver else 1 - side
        face = 2 * axis + held
        return pltpu.make_async_remote_copy(
            src_ref=packed.at[slab(axis, side)],
            dst_ref=halos[axis].at[held],
            send_sem=send_one.at[2 * axis + side],
            recv_sem=recv_one.at[face],
            device_id=beside(axis, side),
            device_id_type=pl.DeviceIdType.MESH,
        )

    def next_copy(axis, side):
        return pltpu.make_async_remote_copy(
            src_ref=mapped.at[slab(axis, 0)],
            dst_ref=nexts[axis],
            send_sem=send_two.at[axis],
            recv_sem=recv_two.at[axis],
            device_id=beside(axis, side),
            device_id_type=pl.DeviceIdType.MESH,
        )

    for axis, side in faces:
        pl.when(exists(axis, side))(lambda a=axis, s=side: halo_copy(a, s, False).start())
    for axis, side in faces:
        pl.when(exists(axis, side))(lambda a=axis, s=side: halo_copy(a, s, True).wait_recv())

    first_product(outer, False)

    images = {}
    for cell in cells:
        images[cell] = []
        for which in range(3):
            summed = jnp.sum(acc[cell + (which,)].T, axis=0, keepdims=True)
            value = row(packed, cell, 3 + which)
            image = (walls[cell][which] * value + summed) * occupied[cell]
            images[cell].append(image)
            mapped[cell + (pl.ds(which, 1),)] = image
        mapped[cell + (pl.ds(3, lanes - 3),)] = jnp.zeros((lanes - 3, width), jnp.float32)

    for axis in range(3):
        if sizes[axis] > 1:
            pl.when(exists(axis, 0))(lambda a=axis: next_copy(a, 0).start())

    for cell in cells:
        spread(image_column, cell, images[cell])

    def other_of(cell, axis):
        there = list(cell)
        if axis is None:
            return packed, cell, mapped, cell
        there[axis] += 1
        if there[axis] < local[axis]:
            return packed, tuple(there), mapped, tuple(there)
        there[axis] = 0
        return halos[axis], (1,) + tuple(there), nexts[axis], tuple(there)

    blocks = [
        key for key in saved
        if key[1] is None or key[0][key[1]] + 1 < local[key[1]] or sizes[key[1]] > 1
    ]

    def second_body(group, carry):
        rows = pl.ds(pl.multiple_of(group * lanes, lanes), lanes)
        result = []
        for (cell, axis), total in zip(blocks, carry):
            place, index, _, _ = other_of(cell, axis)
            slot = slot_of[(cell, axis)]
            delta = [
                column[cell + (which, rows)] - row(place, index, which) for which in range(3)
            ]
            value = [image_column[cell + (which, rows)] for which in range(3)]
            isotropic = iso[slot, rows]
            scaled = dyad[slot, rows] * (
                delta[0] * value[0] + delta[1] * value[1] + delta[2] * value[2]
            )
            result.append(tuple(
                total[which] + isotropic * value[which] + delta[which] * scaled
                for which in range(3)
            ))
        return tuple(result)

    zero = (jnp.zeros((lanes, width), jnp.float32),) * 3
    pushed = lax.fori_loop(0, groups, second_body, (zero,) * len(blocks))

    noise_sq = cross_one = image_sq = wall_sq = jnp.zeros((1, width), jnp.float32)
    for cell in cells:
        for which in range(3):
            value, image = row(packed, cell, 3 + which), images[cell][which]
            noise_sq += value * value
            cross_one += value * image
            image_sq += image * image
            wall_sq += walls[cell][which] * image * image

    own_pairs = jnp.zeros((lanes, width), jnp.float32)
    remote = []
    for (cell, axis), total in zip(blocks, pushed):
        _, _, vector, index = other_of(cell, axis)
        if axis is not None and cell[axis] + 1 == local[axis]:
            remote.append((vector, index, total))
            continue
        weight = 1.0 if axis is None else 2.0
        for which in range(3):
            own_pairs += weight * total[which] * row(vector, index, which)

    for axis in range(3):
        if sizes[axis] > 1:
            pl.when(exists(axis, 1))(lambda a=axis: next_copy(a, 1).wait_recv())

    for vector, index, total in remote:
        for which in range(3):
            own_pairs += 2.0 * total[which] * row(vector, index, which)
    cross_two = wall_sq + jnp.sum(own_pairs, axis=0, keepdims=True)

    sublane = lax.broadcasted_iota(jnp.int32, (lanes, width), 0)
    tile = jnp.where(sublane == 0, noise_sq, 0.0)
    for which, part in enumerate((cross_one, image_sq, cross_two)):
        tile = jnp.where(sublane == which + 1, part, tile)
    reduced = jnp.broadcast_to(jnp.sum(tile, axis=1, keepdims=True), (lanes, width))
    chosen = sublane == lax.broadcasted_iota(jnp.int32, (lanes, width), 1)
    partial = jnp.sum(jnp.where(chosen, reduced, 0.0), axis=0, keepdims=True)

    base = 0
    for number, stage in enumerate(offsets):
        count = len(stage)
        if count == 0:
            continue
        position = {offset: base + order for order, offset in enumerate(stage)}
        own = base + count
        sums[pl.ds(own, 1)] = partial
        copies = []
        for offset in stage:
            back = tuple((sizes[k] - offset[k]) % sizes[k] for k in range(3))
            copy = pltpu.make_async_remote_copy(
                src_ref=sums.at[pl.ds(own, 1)],
                dst_ref=sums.at[pl.ds(position[back], 1)],
                send_sem=send_sum.at[position[offset]],
                recv_sem=recv_sum.at[position[back]],
                device_id=shifted(here, sizes, offset),
                device_id_type=pl.DeviceIdType.MESH,
            )
            copy.start()
            copies.append((offset, copy))
        for offset, _ in copies:
            pltpu.make_async_remote_copy(
                src_ref=sums.at[pl.ds(own, 1)],
                dst_ref=sums.at[pl.ds(position[offset], 1)],
                send_sem=send_sum.at[position[offset]],
                recv_sem=recv_sum.at[position[offset]],
                device_id=shifted(here, sizes, offset),
                device_id_type=pl.DeviceIdType.MESH,
            ).wait_recv()
        partial = jnp.sum(sums[pl.ds(base, count + 1)], axis=0, keepdims=True)
        for _, copy in copies:
            copy.wait_send()
        base += -(-(count + 1) // lanes) * lanes

    def scalar(which):
        return jnp.sum(jnp.where(lane == which, partial, 0.0), axis=1, keepdims=True)

    noise, cross, image_norm, cross_next = (scalar(which) for which in range(4))
    alpha_one = cross / noise
    beta_sq = image_norm / noise - alpha_one * alpha_one
    alpha_two = (
        cross_next - 2.0 * alpha_one * image_norm + alpha_one * alpha_one * cross
    ) / (noise * beta_sq)
    root_det = jnp.sqrt(alpha_one * alpha_two - beta_sq)
    trace_root = jnp.sqrt(alpha_one + alpha_two + 2.0 * root_det)
    image_factor = 1.0 / trace_root
    noise_factor = root_det * image_factor
    for cell in cells:
        out_ref[cell] = (
            noise_factor * packed[cell + (pl.ds(3, 3),)]
            + image_factor * mapped[cell + (pl.ds(0, 3),)]
        )

    for axis, side in faces:
        pl.when(exists(axis, side))(lambda a=axis, s=side: halo_copy(a, s, False).wait_send())
    for axis in range(3):
        if sizes[axis] > 1:
            pl.when(exists(axis, 0))(lambda a=axis: next_copy(a, 0).wait_send())


def shards(sizes, positions, gaussian, counts):
    local, width = positions.shape[:3], positions.shape[-1]
    cells = local[0] * local[1] * local[2]
    f32 = jnp.float32
    vmem = lambda *shape: pltpu.VMEM(shape, f32)
    slabs = [tuple(1 if k == axis else local[k] for k in range(3)) for axis in range(3)]
    rows = sum(
        -(-(len(stage_offsets(sizes, axes)) + 1) // lanes) * lanes for axes in groups_of(sizes)
    )
    sem = lambda count: pltpu.SemaphoreType.DMA((count,))
    return pl.pallas_call(
        functools.partial(kernel, sizes, local, width),
        out_shape=jax.ShapeDtypeStruct(positions.shape, f32),
        in_specs=[
            pl.BlockSpec(memory_space=pltpu.SMEM),
            pl.BlockSpec(memory_space=pltpu.VMEM),
            pl.BlockSpec(memory_space=pltpu.VMEM),
        ],
        out_specs=pl.BlockSpec(memory_space=pltpu.VMEM),
        scratch_shapes=[
            vmem(*local, lanes, width),
            vmem(*local, lanes, width),
            *(vmem(2, *slab, lanes, width) for slab in slabs),
            *(vmem(*slab, lanes, width) for slab in slabs),
            vmem(*local, 3, width, width),
            vmem(*local, 3, width, width),
            vmem(*local, 3, width, width),
            vmem(4 * cells, width, width),
            vmem(4 * cells, width, width),
            vmem(rows, width),
            sem(6), sem(6), sem(3), sem(3), sem(rows), sem(rows),
        ],
        compiler_params=pltpu.CompilerParams(collective_id=0, has_side_effects=True),
    )(counts, positions, gaussian)


def solution(mesh):
    sizes = tuple(mesh.shape[name] for name in names)
    in_specs = (
        P("gx", "gy", "gz", None, None),
        P("gx", "gy", "gz", None, None),
        P("gx", "gy", "gz"),
    )
    out_specs = P("gx", "gy", "gz", None, None)
    return jax.shard_map(
        functools.partial(shards, sizes), mesh=mesh, in_specs=in_specs, out_specs=out_specs,
        check_vma=False,
    )
```

time: 119 us -> 21.5 us (0.18)
  starting transfers between devices: 46.7 us -> 0 us
  blocking collectives: 43.1 us -> 0 us
  Pallas kernels: 0 us -> 18 us
  waiting for transfers between devices: 10.8 us -> 0 us
  other arithmetic: 6.26 us -> 0 us
  between operations: 5.87 us -> 0.01 us
  matrix products: 4.54 us -> 0 us
  local copies, waits for them, and re-layouts: 0.8 us -> 3.14 us
    ppermute x18 -> x0, starting transfers between devices: 46.7 us -> none  [the longest x9 35 us: padded_2(): before = lax.ppermute(last, axis, up)]
    psum x1 -> x0, blocking collectives: 43.1 us -> none  [shards(): lax.psum((jnp.sum(masked * masked), jnp.sum(masked * mapped), jnp.sum(map...]
    pallas_call x0 -> x1, Pallas kernels: none -> 18 us  [shards(): pl.pallas_call(functools.partial(kernel, sizes, local, width), out_shape=...]
    ppermute x18 -> x0, waiting for transfers between devices: 10.8 us -> none  [the longest x9 8.64 us: padded_2(): after = lax.ppermute(leading, axis, down)]
    reduce_sum x7 -> x0, other arithmetic: 4.61 us -> none  [the longest x2 1.81 us: pair_terms(): along_pair = jnp.sum(offset_vec * (dyadic * projected)[:, None], axis=3)]
    dot_general x14 -> x0, matrix products: 4.54 us -> none  [pair_terms(): jnp.einsum('bij,bcj->bci', isotropic, values, precision=lax.Precision.HIG...]
    pallas_call x0 -> x1, local copies, waits for them, and re-layouts: none -> 1.26 us  [shards(): pl.pallas_call(functools.partial(kernel, sizes, local, width), out_shape=...]
    unnamed x8 -> x4, local copies, waits for them, and re-layouts: 0.67 us -> 1.88 us
  transfers between devices with their start and end apart: 18 -> 0, of which waited for: 4 -> 0; matrix products, arithmetic and copies ran while one was open for 1% -> 0% of each run, Pallas kernels for 0% -> 0%
where the time goes in v1:
time: 21.5 us; the launch traced here: 21.2 us
  Pallas kernels  18 us (84%)
  local copies, waits for them, and re-layouts  3.14 us (15%)
    pallas_call x1, Pallas kernels, shards(): pl.pallas_call(functools.partial(kernel, sizes, local, width), out_shape=...  18 us
    unnamed x4, local copies, waits for them, and re-layouts  1.88 us
    pallas_call x1, local copies, waits for them, and re-layouts, shards(): pl.pallas_call(functools.partial(kernel, sizes, local, width), out_shape=...  1.26 us

profile of v1, /device:TPU:0, one launch (start us, length us, event | category | flops | bytes accessed | tf_op | source)
XLA Modules:
  0.0 21.2 jit_solution(7863781631462194588)
XLA Ops:
  0.0 0.0 copy-start
  0.0 1.3 %copy.4.pos_ref = f32[1,1,2,3,128]{4,3,2,1,0:T(4,128)} copy(f32[1,1,2,3,128]{4,2,3,1,0:T(2,128)} %param.3) | data formatting | bytes 6144 | tf_op args[0]
  1.3 0.0 copy-done
  1.3 0.6 %copy.5.gauss_ref = f32[1,1,2,3,128]{4,3,2,1,0:T(4,128)} copy(f32[1,1,2,3,128]{4,2,3,1,0:T(2,128)S(1)} %copy-done) | data formatting | bytes 6144 | tf_op args[1]
  1.9 18.0 %shard_map.37 = f32[1,1,2,3,128]{4,3,2,1,0:T(4,128)} custom-call(s32[1,1,2]{2,1,0:T(1,128)} %counts_ref.1, f32[1,1,2,3,128]{4,3,2,1,0:T(4,128)} %copy.4.pos_ref, f32[1,1,2,3,128]{4,3,2,1,0:T(4,128)} %copy.5.gauss_ref), custom_call_target="tpu_custom_call" | custom-call | tf_op jit(solution)/shard_map/pallas_call | solution.py:377
  19.9 1.3 %copy.6 = f32[1,1,2,3,128]{4,2,3,1,0:T(2,128)} copy(f32[1,1,2,3,128]{4,3,2,1,0:T(4,128)} %shard_map.37) | data formatting | bytes 6144 | tf_op jit(solution)/shard_map/pallas_call | solution.py:377
Async XLA Ops:
  0.0 1.3 %copy-start = (f32[1,1,2,3,128]{4,2,3,1,0:T(2,128)S(1)}, f32[1,1,2,3,128]{4,2,3,1,0:T(2,128)}, u32[]{:S(2)}) copy-start(f32[1,1,2,3,128]{4,2,3,1,0:T(2,128)} %param.4) | copy-start | bytes 9220

commit v2 on v1

--- a/solution.py
+++ b/solution.py
@@ -53,8 +53,8 @@
 
 
 def kernel(
-    sizes, local, width, counts_ref, pos_ref, gauss_ref, out_ref,
-    packed, mapped, halo_x, halo_y, halo_z, next_x, next_y, next_z,
+    sizes, local, width, counts_hbm, pos_hbm, gauss_hbm, out_ref,
+    counts_ref, pos_ref, gauss_ref, load_sem, packed, mapped, halo_x, halo_y, halo_z, next_x, next_y, next_z,
     column, image_column, acc, iso, dyad, sums,
     send_one, recv_one, send_two, recv_two, send_sum, recv_sum,
 ):
@@ -76,6 +76,15 @@
 
     def beside(axis, side):
         return {names[axis]: here[axis] + (1 if side else -1)}
+
+    loads = [
+        pltpu.make_async_copy(source, target, load_sem.at[order])
+        for order, (source, target) in enumerate(
+            ((pos_hbm, pos_ref), (gauss_hbm, gauss_ref), (counts_hbm, counts_ref))
+        )
+    ]
+    for load in loads:
+        load.start()
 
     zero_tile = jnp.zeros((lanes, width), jnp.float32)
     tile_row = lax.broadcasted_iota(jnp.int32, (lanes, width), 0)
@@ -98,15 +107,18 @@
             device_id_type=pl.DeviceIdType.MESH,
         )
 
+    for load in loads:
+        load.wait()
     lane = lax.broadcasted_iota(jnp.int32, (1, width), 1)
     occupied, walls = {}, {}
     for cell in cells:
         occupied[cell] = (lane < counts_ref[cell]).astype(jnp.float32)
-        position = pos_ref[cell]
-        packed[cell + (pl.ds(0, 3),)] = position
-        packed[cell + (pl.ds(3, 3),)] = gauss_ref[cell] * occupied[cell]
+        for which in range(3):
+            from_array = cell[:2] + (which, pl.ds(cell[2], 1))
+            packed[cell + (pl.ds(which, 1),)] = pos_ref[from_array]
+            packed[cell + (pl.ds(3 + which, 1),)] = gauss_ref[from_array] * occupied[cell]
         packed[cell + (pl.ds(6, 2),)] = jnp.zeros((2, width), jnp.float32)
-        walls[cell] = wall_mobility(position[2:3])
+        walls[cell] = wall_mobility(packed[cell + (pl.ds(2, 1),)])
 
     def row(ref, index, which):
         return ref[index + (pl.ds(which, 1),)]
@@ -352,10 +364,11 @@
     image_factor = 1.0 / trace_root
     noise_factor = root_det * image_factor
     for cell in cells:
-        out_ref[cell] = (
-            noise_factor * packed[cell + (pl.ds(3, 3),)]
-            + image_factor * mapped[cell + (pl.ds(0, 3),)]
-        )
+        for which in range(3):
+            out_ref[cell[:2] + (which, pl.ds(cell[2], 1))] = (
+                noise_factor * row(packed, cell, 3 + which)
+                + image_factor * row(mapped, cell, which)
+            )
 
     for axis, side in faces:
         pl.when(exists(axis, side))(lambda a=axis, s=side: halo_copy(a, s, False).wait_send())
@@ -369,21 +382,23 @@
     cells = local[0] * local[1] * local[2]
     f32 = jnp.float32
     vmem = lambda *shape: pltpu.VMEM(shape, f32)
+    sem = lambda count: pltpu.SemaphoreType.DMA((count,))
     slabs = [tuple(1 if k == axis else local[k] for k in range(3)) for axis in range(3)]
     rows = sum(
         -(-(len(stage_offsets(sizes, axes)) + 1) // lanes) * lanes for axes in groups_of(sizes)
     )
-    sem = lambda count: pltpu.SemaphoreType.DMA((count,))
-    return pl.pallas_call(
+    order = (0, 1, 3, 2, 4)
+    positions, gaussian = (jnp.transpose(array, order) for array in (positions, gaussian))
+    result = pl.pallas_call(
         functools.partial(kernel, sizes, local, width),
         out_shape=jax.ShapeDtypeStruct(positions.shape, f32),
-        in_specs=[
-            pl.BlockSpec(memory_space=pltpu.SMEM),
-            pl.BlockSpec(memory_space=pltpu.VMEM),
-            pl.BlockSpec(memory_space=pltpu.VMEM),
-        ],
+        in_specs=[pl.BlockSpec(memory_space=pltpu.HBM)] * 3,
         out_specs=pl.BlockSpec(memory_space=pltpu.VMEM),
         scratch_shapes=[
+            pltpu.SMEM(counts.shape, jnp.int32),
+            vmem(*positions.shape),
+            vmem(*positions.shape),
+            sem(3),
             vmem(*local, lanes, width),
             vmem(*local, lanes, width),
             *(vmem(2, *slab, lanes, width) for slab in slabs),
@@ -398,6 +413,7 @@
         ],
         compiler_params=pltpu.CompilerParams(collective_id=0, has_side_effects=True),
     )(counts, positions, gaussian)
+    return jnp.transpose(result, order)
 
 
 def solution(mesh):

time: 21.5 us -> 18.8 us (0.87)
  local copies, waits for them, and re-layouts: 3.14 us -> 1.26 us
  Pallas kernels: 18 us -> 17.3 us
    pallas_call x1 -> x0, local copies, waits for them, and re-layouts: 1.26 us -> none  [shards(): pl.pallas_call(functools.partial(kernel, sizes, local, width), out_shape=...]
    pallas_call x1, Pallas kernels: 18 us -> 17.3 us  [shards(): pl.pallas_call(functools.partial(kernel, sizes, local, width), out_shape=...]
    unnamed x4 -> x1, local copies, waits for them, and re-layouts: 1.88 us -> 1.26 us
where the time goes in v2:
time: 18.8 us; the launch traced here: 18.6 us
  Pallas kernels  17.3 us (92%)
  local copies, waits for them, and re-layouts  1.26 us (7%)
    pallas_call x1, Pallas kernels, shards(): pl.pallas_call(functools.partial(kernel, sizes, local, width), out_shape=...  17.3 us
    unnamed x1, local copies, waits for them, and re-layouts  1.26 us

profile of v2, /device:TPU:0, one launch (start us, length us, event | category | flops | bytes accessed | tf_op | source)
XLA Modules:
  0.0 18.6 jit_solution(15118978328518418443)
XLA Ops:
  0.0 17.3 %shard_map.37 = f32[1,1,3,2,128]{4,3,2,1,0:T(2,128)} custom-call(s32[1,1,2]{2,1,0:T(1,128)} %counts_hbm.1, f32[1,1,3,2,128]{4,3,2,1,0:T(2,128)} %bitcast.4, f32[1,1,3,2,128]{4,3,2,1,0:T(2,128)} %bitcast.5), custom_call_target="tpu_custom_call" | custom-call | tf_op jit(solution)/shard_map/pallas_call | solution.py:392
  17.3 1.3 %copy.5 = f32[1,1,2,3,128]{4,2,3,1,0:T(2,128)} copy(f32[1,1,2,3,128]{4,2,3,1,0:T(2,128)} %bitcast.3) | data formatting | bytes 6144

commit v3 on v2

--- a/solution.py
+++ b/solution.py
@@ -25,10 +25,20 @@
     return [offset for offset in itertools.product(*ranges) if any(offset)]
 
 
-def shifted(here, sizes, offset):
-    return tuple(
-        lax.rem(here[k] + offset[k], sizes[k]) if offset[k] else here[k] for k in range(3)
-    )
+def barrier_offsets(sizes):
+    stages = groups_of(sizes)
+    if len(stages) > 1:
+        return [offset for axes in stages for offset in stage_offsets(sizes, axes)], []
+    plane = stage_offsets(sizes, (0, 1))
+    return plane + stage_offsets(sizes, (2,)), plane
+
+
+def around(here, sizes):
+    table = []
+    for k in range(3):
+        ahead = [here[k] + step for step in range(sizes[k])]
+        table.append([jnp.where(at >= sizes[k], at - sizes[k], at) for at in ahead])
+    return table
 
 
 def wall_mobility(height):
@@ -56,7 +66,7 @@
     sizes, local, width, counts_hbm, pos_hbm, gauss_hbm, out_ref,
     counts_ref, pos_ref, gauss_ref, load_sem, packed, mapped, halo_x, halo_y, halo_z, next_x, next_y, next_z,
     column, image_column, acc, iso, dyad, sums,
-    send_one, recv_one, send_two, recv_two, send_sum, recv_sum,
+    send_one, recv_one, send_two, recv_two, send_sum, recv_sum, told_sem,
 ):
     here = tuple(lax.axis_index(name) for name in names)
     cells = list(itertools.product(*(range(size) for size in local)))
@@ -85,6 +95,19 @@
     ]
     for load in loads:
         load.start()
+
+    ring = around(here, sizes)
+
+    def shifted(offset):
+        return tuple(ring[k][offset[k]] for k in range(3))
+
+    barrier = pltpu.get_barrier_semaphore()
+    peers, told = barrier_offsets(sizes)
+    for offset in peers:
+        pl.semaphore_signal(
+            barrier, inc=1, device_id=shifted(offset),
+            device_id_type=pl.DeviceIdType.MESH,
+        )
 
     zero_tile = jnp.zeros((lanes, width), jnp.float32)
     tile_row = lax.broadcasted_iota(jnp.int32, (lanes, width), 0)
@@ -98,14 +121,6 @@
                     if side:
                         nexts[axis][cell] = zero_tile
             pl.when(jnp.logical_not(exists(axis, side)))(clear)
-
-    barrier = pltpu.get_barrier_semaphore()
-    peers = [offset for stage in offsets for offset in stage]
-    for offset in peers:
-        pl.semaphore_signal(
-            barrier, inc=1, device_id=shifted(here, sizes, offset),
-            device_id_type=pl.DeviceIdType.MESH,
-        )
 
     for load in loads:
         load.wait()
@@ -217,6 +232,10 @@
 
     for axis, side in faces:
         pl.when(exists(axis, side))(lambda a=axis, s=side: halo_copy(a, s, False).start())
+    for offset in told:
+        pl.semaphore_signal(
+            told_sem, inc=1, device_id=shifted(offset), device_id_type=pl.DeviceIdType.MESH
+        )
     for axis, side in faces:
         pl.when(exists(axis, side))(lambda a=axis, s=side: halo_copy(a, s, True).wait_recv())
 
@@ -315,6 +334,8 @@
     chosen = sublane == lax.broadcasted_iota(jnp.int32, (lanes, width), 1)
     partial = jnp.sum(jnp.where(chosen, reduced, 0.0), axis=0, keepdims=True)
 
+    if told:
+        pl.semaphore_wait(told_sem, len(told))
     base = 0
     for number, stage in enumerate(offsets):
         count = len(stage)
@@ -331,7 +352,7 @@
                 dst_ref=sums.at[pl.ds(position[back], 1)],
                 send_sem=send_sum.at[position[offset]],
                 recv_sem=recv_sum.at[position[back]],
-                device_id=shifted(here, sizes, offset),
+                device_id=shifted(offset),
                 device_id_type=pl.DeviceIdType.MESH,
             )
             copy.start()
@@ -342,7 +363,7 @@
                 dst_ref=sums.at[pl.ds(position[offset], 1)],
                 send_sem=send_sum.at[position[offset]],
                 recv_sem=recv_sum.at[position[offset]],
-                device_id=shifted(here, sizes, offset),
+                device_id=shifted(offset),
                 device_id_type=pl.DeviceIdType.MESH,
             ).wait_recv()
         partial = jnp.sum(sums[pl.ds(base, count + 1)], axis=0, keepdims=True)
@@ -391,7 +412,7 @@
     positions, gaussian = (jnp.transpose(array, order) for array in (positions, gaussian))
     result = pl.pallas_call(
         functools.partial(kernel, sizes, local, width),
-        out_shape=jax.ShapeDtypeStruct(positions.shape, f32),
+        out_shape=pltpu.VMEM(positions.shape, f32),
         in_specs=[pl.BlockSpec(memory_space=pltpu.HBM)] * 3,
         out_specs=pl.BlockSpec(memory_space=pltpu.VMEM),
         scratch_shapes=[
@@ -409,7 +430,7 @@
             vmem(4 * cells, width, width),
             vmem(4 * cells, width, width),
             vmem(rows, width),
-            sem(6), sem(6), sem(3), sem(3), sem(rows), sem(rows),
+            sem(6), sem(6), sem(3), sem(3), sem(rows), sem(rows), pltpu.SemaphoreType.REGULAR,
         ],
         compiler_params=pltpu.CompilerParams(collective_id=0, has_side_effects=True),
     )(counts, positions, gaussian)

time: 18.8 us -> 17.4 us (0.926)
  Pallas kernels: 17.3 us -> 16.6 us
  local copies, waits for them, and re-layouts: 1.26 us -> 0.58 us
    pallas_call x1, Pallas kernels: 17.3 us -> 16.6 us  [shards(): pl.pallas_call(functools.partial(kernel, sizes, local, width), out_shape=...]
    unnamed x1, local copies, waits for them, and re-layouts: 1.26 us -> 0.58 us
where the time goes in v3:
time: 17.4 us; the launch traced here: 17.2 us
  Pallas kernels  16.6 us (95%)
  local copies, waits for them, and re-layouts  0.58 us (3%)
    pallas_call x1, Pallas kernels, shards(): pl.pallas_call(functools.partial(kernel, sizes, local, width), out_shape=...  16.6 us
    unnamed x1, local copies, waits for them, and re-layouts  0.58 us

profile of v3, /device:TPU:0, one launch (start us, length us, event | category | flops | bytes accessed | tf_op | source)
XLA Modules:
  0.0 17.2 jit_solution(8228612243143414833)
XLA Ops:
  0.0 16.6 %shard_map.37 = f32[1,1,3,2,128]{4,3,2,1,0:T(2,128)S(1)} custom-call(s32[1,1,2]{2,1,0:T(1,128)} %counts_hbm.1, f32[1,1,3,2,128]{4,3,2,1,0:T(2,128)} %bitcast.4, f32[1,1,3,2,128]{4,3,2,1,0:T(2,128)} %bitcast.5), custom_call_target="tpu_custom_call" | custom-call | tf_op jit(solution)/shard_map/pallas_call | solution.py:413
  16.7 0.6 %copy.5 = f32[1,1,2,3,128]{4,2,3,1,0:T(2,128)} copy(f32[1,1,2,3,128]{4,2,3,1,0:T(2,128)S(1)} %bitcast.3) | data formatting | bytes 6144

commit v4 on v3

--- a/solution.py
+++ b/solution.py
@@ -22,7 +22,9 @@
 
 def stage_offsets(sizes, axes):
     ranges = [range(sizes[k]) if k in axes else range(1) for k in range(3)]
-    return [offset for offset in itertools.product(*ranges) if any(offset)]
+    away = lambda offset: sum(min(o, size - o) for o, size in zip(offset, sizes))
+    found = [offset for offset in itertools.product(*ranges) if any(offset)]
+    return sorted(found, key=away, reverse=True)
 
 
 def barrier_offsets(sizes):
@@ -142,9 +144,6 @@
         for which in range(3):
             full = jnp.broadcast_to(values[which], (width, width))
             ref[cell + (which,)] = full.T
-
-    for cell in cells:
-        spread(column, cell, [row(packed, cell, which) for which in range(3)])
 
     def source_of(cell, axis, side):
         there = list(cell)
@@ -204,8 +203,6 @@
 
         lax.fori_loop(0, groups, body, 0)
 
-    first_product(inner, True)
-
     pl.semaphore_wait(barrier, len(peers))
 
     def halo_copy(axis, side, receiver):
@@ -236,6 +233,11 @@
         pl.semaphore_signal(
             told_sem, inc=1, device_id=shifted(offset), device_id_type=pl.DeviceIdType.MESH
         )
+    for cell in cells:
+        spread(column, cell, [row(packed, cell, which) for which in range(3)])
+
+    first_product(inner, True)
+
     for axis, side in faces:
         pl.when(exists(axis, side))(lambda a=axis, s=side: halo_copy(a, s, True).wait_recv())
 

time: 17.4 us -> 17.4 us (level)
  no operation moved by 1% of the time
where the time goes in v4:
time: 17.4 us; the launch traced here: 17.2 us
  Pallas kernels  16.6 us (95%)
  local copies, waits for them, and re-layouts  0.58 us (3%)
    pallas_call x1, Pallas kernels, shards(): pl.pallas_call(functools.partial(kernel, sizes, local, width), out_shape=...  16.6 us
    unnamed x1, local copies, waits for them, and re-layouts  0.58 us

profile of v4, /device:TPU:0, one launch (start us, length us, event | category | flops | bytes accessed | tf_op | source)
XLA Modules:
  0.0 17.2 jit_solution(4379015232653439496)
XLA Ops:
  0.0 16.6 %shard_map.37 = f32[1,1,3,2,128]{4,3,2,1,0:T(2,128)S(1)} custom-call(s32[1,1,2]{2,1,0:T(1,128)} %counts_hbm.1, f32[1,1,3,2,128]{4,3,2,1,0:T(2,128)} %bitcast.4, f32[1,1,3,2,128]{4,3,2,1,0:T(2,128)} %bitcast.5), custom_call_target="tpu_custom_call" | custom-call | tf_op jit(solution)/shard_map/pallas_call | solution.py:415
  16.6 0.6 %copy.5 = f32[1,1,2,3,128]{4,2,3,1,0:T(2,128)} copy(f32[1,1,2,3,128]{4,2,3,1,0:T(2,128)S(1)} %bitcast.3) | data formatting | bytes 6144

commit v5 on v4

--- a/solution.py
+++ b/solution.py
@@ -27,12 +27,14 @@
     return sorted(found, key=away, reverse=True)
 
 
-def barrier_offsets(sizes):
+def entry_plan(sizes):
     stages = groups_of(sizes)
     if len(stages) > 1:
-        return [offset for axes in stages for offset in stage_offsets(sizes, axes)], []
+        return [offset for axes in stages for offset in stage_offsets(sizes, axes)], False, []
+    near = 1 < sizes[2] <= 4
+    lines = stage_offsets(sizes, (0,)) + stage_offsets(sizes, (1,))
     plane = stage_offsets(sizes, (0, 1))
-    return plane + stage_offsets(sizes, (2,)), plane
+    return (lines if near else plane + stage_offsets(sizes, (2,))), near, plane
 
 
 def around(here, sizes):
@@ -68,7 +70,7 @@
     sizes, local, width, counts_hbm, pos_hbm, gauss_hbm, out_ref,
     counts_ref, pos_ref, gauss_ref, load_sem, packed, mapped, halo_x, halo_y, halo_z, next_x, next_y, next_z,
     column, image_column, acc, iso, dyad, sums,
-    send_one, recv_one, send_two, recv_two, send_sum, recv_sum, told_sem,
+    send_one, recv_one, send_two, recv_two, send_sum, recv_sum, told_sem, line_sem,
 ):
     here = tuple(lax.axis_index(name) for name in names)
     cells = list(itertools.product(*(range(size) for size in local)))
@@ -104,7 +106,12 @@
         return tuple(ring[k][offset[k]] for k in range(3))
 
     barrier = pltpu.get_barrier_semaphore()
-    peers, told = barrier_offsets(sizes)
+    peers, near, told = entry_plan(sizes)
+    if near:
+        for side in range(2):
+            pl.when(exists(2, side))(lambda s=side: pl.semaphore_signal(
+                barrier, inc=1, device_id=beside(2, s), device_id_type=pl.DeviceIdType.MESH
+            ))
     for offset in peers:
         pl.semaphore_signal(
             barrier, inc=1, device_id=shifted(offset),
@@ -203,7 +210,8 @@
 
         lax.fori_loop(0, groups, body, 0)
 
-    pl.semaphore_wait(barrier, len(peers))
+    along_z = sum(jnp.where(exists(2, side), 1, 0) for side in range(2))
+    pl.semaphore_wait(barrier, len(peers) + along_z if near else len(peers))
 
     def halo_copy(axis, side, receiver):
         held = side if receiver else 1 - side
@@ -229,10 +237,6 @@
 
     for axis, side in faces:
         pl.when(exists(axis, side))(lambda a=axis, s=side: halo_copy(a, s, False).start())
-    for offset in told:
-        pl.semaphore_signal(
-            told_sem, inc=1, device_id=shifted(offset), device_id_type=pl.DeviceIdType.MESH
-        )
     for cell in cells:
         spread(column, cell, [row(packed, cell, which) for which in range(3)])
 
@@ -240,6 +244,12 @@
 
     for axis, side in faces:
         pl.when(exists(axis, side))(lambda a=axis, s=side: halo_copy(a, s, True).wait_recv())
+
+    if near:
+        for side in range(2):
+            pl.when(exists(2, side))(lambda s=side: pl.semaphore_signal(
+                line_sem, inc=1, device_id=beside(2, s), device_id_type=pl.DeviceIdType.MESH
+            ))
 
     first_product(outer, False)
 
@@ -257,6 +267,13 @@
     for axis in range(3):
         if sizes[axis] > 1:
             pl.when(exists(axis, 0))(lambda a=axis: next_copy(a, 0).start())
+
+    if near:
+        pl.semaphore_wait(line_sem, along_z)
+    for offset in told:
+        pl.semaphore_signal(
+            told_sem, inc=1, device_id=shifted(offset), device_id_type=pl.DeviceIdType.MESH
+        )
 
     for cell in cells:
         spread(image_column, cell, images[cell])
@@ -432,7 +449,7 @@
             vmem(4 * cells, width, width),
             vmem(4 * cells, width, width),
             vmem(rows, width),
-            sem(6), sem(6), sem(3), sem(3), sem(rows), sem(rows), pltpu.SemaphoreType.REGULAR,
+            sem(6), sem(6), sem(3), sem(3), sem(rows), sem(rows), pltpu.SemaphoreType.REGULAR, pltpu.SemaphoreType.REGULAR,
         ],
         compiler_params=pltpu.CompilerParams(collective_id=0, has_side_effects=True),
     )(counts, positions, gaussian)

time: 17.4 us -> 17.4 us (level)
  no operation moved by 1% of the time
where the time goes in v5:
time: 17.4 us; the launch traced here: 17.2 us
  Pallas kernels  16.6 us (95%)
  local copies, waits for them, and re-layouts  0.58 us (3%)
    pallas_call x1, Pallas kernels, shards(): pl.pallas_call(functools.partial(kernel, sizes, local, width), out_shape=...  16.6 us
    unnamed x1, local copies, waits for them, and re-layouts  0.58 us

profile of v5, /device:TPU:0, one launch (start us, length us, event | category | flops | bytes accessed | tf_op | source)
XLA Modules:
  0.0 17.2 jit_solution(1796243252739157088)
XLA Ops:
  0.0 16.6 %shard_map.37 = f32[1,1,3,2,128]{4,3,2,1,0:T(2,128)S(1)} custom-call(s32[1,1,2]{2,1,0:T(1,128)} %counts_hbm.1, f32[1,1,3,2,128]{4,3,2,1,0:T(2,128)} %bitcast.4, f32[1,1,3,2,128]{4,3,2,1,0:T(2,128)} %bitcast.5), custom_call_target="tpu_custom_call" | custom-call | tf_op jit(solution)/shard_map/pallas_call | solution.py:432
  16.6 0.6 %copy.5 = f32[1,1,2,3,128]{4,2,3,1,0:T(2,128)} copy(f32[1,1,2,3,128]{4,2,3,1,0:T(2,128)S(1)} %bitcast.3) | data formatting | bytes 6144

commit v6 on v5

--- a/solution.py
+++ b/solution.py
@@ -208,7 +208,7 @@
                     acc[cell + (which, rows)] = total[which]
             return carry
 
-        lax.fori_loop(0, groups, body, 0)
+        lax.fori_loop(0, groups, body, 0, unroll=4)
 
     along_z = sum(jnp.where(exists(2, side), 1, 0) for side in range(2))
     pl.semaphore_wait(barrier, len(peers) + along_z if near else len(peers))
@@ -314,7 +314,7 @@
         return tuple(result)
 
     zero = (jnp.zeros((lanes, width), jnp.float32),) * 3
-    pushed = lax.fori_loop(0, groups, second_body, (zero,) * len(blocks))
+    pushed = lax.fori_loop(0, groups, second_body, (zero,) * len(blocks), unroll=4)
 
     noise_sq = cross_one = image_sq = wall_sq = jnp.zeros((1, width), jnp.float32)
     for cell in cells:

time: 17.4 us -> 17.2 us (0.989)
  no operation moved by 1% of the time
where the time goes in v6:
time: 17.2 us; the launch traced here: 17.1 us
  Pallas kernels  16.5 us (96%)
  local copies, waits for them, and re-layouts  0.58 us (3%)
    pallas_call x1, Pallas kernels, shards(): pl.pallas_call(functools.partial(kernel, sizes, local, width), out_shape=...  16.5 us
    unnamed x1, local copies, waits for them, and re-layouts  0.58 us

profile of v6, /device:TPU:0, one launch (start us, length us, event | category | flops | bytes accessed | tf_op | source)
XLA Modules:
  0.0 17.1 jit_solution(16404558450425555760)
XLA Ops:
  0.0 16.5 %shard_map.37 = f32[1,1,3,2,128]{4,3,2,1,0:T(2,128)S(1)} custom-call(s32[1,1,2]{2,1,0:T(1,128)} %counts_hbm.1, f32[1,1,3,2,128]{4,3,2,1,0:T(2,128)} %bitcast.4, f32[1,1,3,2,128]{4,3,2,1,0:T(2,128)} %bitcast.5), custom_call_target="tpu_custom_call" | custom-call | tf_op jit(solution)/shard_map/pallas_call | solution.py:432
  16.5 0.6 %copy.5 = f32[1,1,2,3,128]{4,2,3,1,0:T(2,128)} copy(f32[1,1,2,3,128]{4,2,3,1,0:T(2,128)S(1)} %bitcast.3) | data formatting | bytes 6144
